TPU v7x, 512 devices: a whole 4x8x8 slice. The times are simulated.
512 devices in a mesh: pair: 64 (over z, y), split: 8 (over x, core).
Axes of the slice: x: 4, y: 8, z: 8, core: 2. Of those that a mesh axis runs over, the one named last changes fastest.
Arguments:
- descriptors: bfloat16 [64, 1024, 256], P('pair', 'split'), as said below
- points: bfloat16 [64, 3, 1024], P('pair', None, 'split'), may hold values from -6 to 6
- normals: bfloat16 [64, 3, 1024], P('pair', None, 'split'), may hold values from -6 to 6
- pair_list: int32 [1536, 2], replicated, may hold values from 0 to 63, as said below
- intersection: int32 [1536], P('pair'), may hold values from 256 to 1024
- pose_index: int32 [64], replicated, may hold values from 0 to 63, each once
Outputs:
- pair_cross: float32 [1536, 6, 6], P('pair')
- pose_hessian: float32 [64, 6, 6], P('pair')
- pose_gradient: float32 [64, 6], P('pair')
Inputs may be any that keep to these rules, and one draw needn't show every extreme that they name: `descriptors`: values stay within -24 to 24. `pair_list`: task k's source scan is scan k // 24. The owner of a scan s is s; a task's target has another owner than its source. Among the 24 tasks of one aligned block (tasks k // 24 alike), no owner holds the targets of more than 1 of them, and some owner holds exactly 1.
All inputs are finite; a program needn't handle non-finite values.
Results may differ from a plain program's by a relative error of at most 0.0003.
Values may be sent and summed in bfloat16 or wider, within the bound.
No kernel may reach another device: no remote copies, remote signals or barrier semaphores. Data moves between devices by JAX's collectives and lax.ppermute only.
A program may use at most 64 MiB of HBM per device.

v0:
```python
import jax
import jax.numpy as jnp
from jax import lax
from jax.sharding import PartitionSpec as P

task_group = 4


def rows_first(arrays, axis, dims):
    turned = [jnp.moveaxis(a, dim, 0) for a, dim in zip(arrays, dims)]
    both = jnp.concatenate([t.reshape(len(t), -1) for t in turned], axis=1)
    out, at, gathered = (lax.all_gather(both, axis, axis=0, tiled=True), 0, [])
    for t, dim in zip(turned, dims):
        share = out[:, at : at + t[0].size].reshape(-1, *t.shape[1:])
        gathered.append(jnp.moveaxis(share, 0, dim))
        at += t[0].size
    return tuple(gathered)


def sent_together(arrays, axis, split_dim, concat_dim, along):
    ends, at = ([], 0)
    for a in arrays[:-1]:
        at += a.shape[along]
        ends.append(at)
    both = jnp.concatenate(arrays, axis=along)
    return tuple(
        jnp.split(
            lax.all_to_all(both, axis, split_axis=split_dim, concat_axis=concat_dim, tiled=True),
            ends,
            axis=along,
        )
    )


def copy_for_each(shard, axis):
    copies = jnp.broadcast_to(shard, (lax.axis_size(axis), *shard.shape))
    return lax.all_to_all(copies, axis, split_axis=0, concat_axis=0, tiled=True)


def of_everyone(shard, axis):
    everything = copy_for_each(shard, axis)
    return jnp.sum(everything, axis=0)


def in_one(arrays, axis):
    ends = [0]
    for a in arrays:
        ends.append(ends[-1] + a.size)
    total = of_everyone(jnp.concatenate([a.ravel() for a in arrays]), axis)
    return tuple((total[b:e].reshape(a.shape) for a, b, e in zip(arrays, ends, ends[1:])))


def in_blocks(shard, dim, size):
    before, after = (shard.shape[:dim], shard.shape[dim + 1 :])
    return jnp.moveaxis(shard.reshape(*before, size, -1, *after), dim, 0)


def sent_and_summed(shard, axis, dim):
    pieces = in_blocks(shard, dim, lax.axis_size(axis))
    arrived = lax.all_to_all(pieces, axis, split_axis=0, concat_axis=0, tiled=True)
    return arrived.sum(axis=0)


def side_by_side(arrays, axis, dim, along):
    both = jnp.concatenate(arrays, axis=along)
    out, at, gathered = (sent_and_summed(both, axis, dim), 0, [])
    for a in arrays:
        gathered.append(lax.slice_in_dim(out, at, at + a.shape[along], axis=along))
        at += a.shape[along]
    return tuple(gathered)


def cross_second(left_vec, right_vec):
    return jnp.stack(
        [
            left_vec[:, 1] * right_vec[:, 2] - left_vec[:, 2] * right_vec[:, 1],
            left_vec[:, 2] * right_vec[:, 0] - left_vec[:, 0] * right_vec[:, 2],
            left_vec[:, 0] * right_vec[:, 1] - left_vec[:, 1] * right_vec[:, 0],
        ],
        axis=1,
    )


def assemble(softened, source, row_seen, counts, all_rows):
    highest = lax.Precision.HIGHEST
    matched = softened[:, :3]
    normal = softened[:, 3:]
    weight = (row_seen[None, :] < counts[:, None]).astype(jnp.float32)
    jacobian = jnp.concatenate(
        [cross_second(source, normal), normal, -cross_second(matched, normal), -normal], axis=1
    )
    residual = jnp.sum(normal * (source - matched), axis=1)
    weighted = jacobian * weight[:, None, :]
    hessian = jnp.einsum("tan,tbn->tab", weighted, jacobian, precision=highest) / all_rows
    gradient = jnp.einsum("tan,tn->ta", weighted, residual, precision=highest) / all_rows
    return (hessian, gradient)


def per_device(descriptors, points, normals, pair_list, intersection, pose_index):
    highest = lax.Precision.HIGHEST
    scan_dev, block_rows, feature_width = descriptors.shape
    split_count = lax.axis_size("split")
    own_index = lax.axis_index("pair")
    all_rows = block_rows * split_count
    task_count = intersection.shape[0]
    my_pairs = lax.dynamic_slice_in_dim(pair_list, own_index * task_count, task_count, 0)
    sources = my_pairs[:, 0] - own_index * scan_dev
    targets = my_pairs[:, 1]
    geometry = jnp.concatenate([points, normals], axis=1)
    source_desc, source_points = rows_first((descriptors, points), "split", (1, 2))
    target_desc, target_geometry = (
        lax.all_gather(descriptors, "pair", axis=0, tiled=True),
        lax.all_gather(geometry, "pair", axis=0, tiled=True),
    )
    score_scale = feature_width ** (-0.5)
    group_count = task_count // task_group

    def attend(indices):
        source_ids, tile_ids = indices
        queries = source_desc[source_ids]
        key_rows = target_desc[tile_ids]
        tile_geometry = target_geometry[tile_ids].astype(jnp.float32)
        scores = (
            jnp.einsum("gic,gjc->gij", queries, key_rows, preferred_element_type=jnp.float32)
            * score_scale
        )
        maxima = jnp.max(scores, axis=2)
        exponent = jnp.exp(scores - maxima[:, :, None])
        totals = jnp.sum(exponent, axis=2)
        moment = jnp.einsum("gij,gdj->gdi", exponent, tile_geometry, precision=highest)
        return (maxima, totals, moment)

    maxima, totals, moment = lax.map(
        attend, (sources.reshape(group_count, task_group), targets.reshape(group_count, task_group))
    )
    maxima = maxima.reshape(task_count, all_rows)
    totals = totals.reshape(task_count, all_rows)
    moment = moment.reshape(task_count, 6, all_rows)
    maxima_parts = maxima.reshape(task_count, 1, split_count, block_rows)
    totals_parts = totals.reshape(task_count, 1, split_count, block_rows)
    moment_parts = moment.reshape(task_count, 6, split_count, block_rows)
    maxima_parts, totals_parts, moment_parts = sent_together(
        (maxima_parts, totals_parts, moment_parts), "split", 2, 2, 1
    )
    highest_score = jnp.max(maxima_parts, axis=2)
    factor = jnp.exp(maxima_parts - highest_score[:, :, None, :])
    totals_row = jnp.sum(totals_parts * factor, axis=2)
    moment_row = jnp.sum(moment_parts * factor, axis=2)
    softened = moment_row / totals_row
    row_seen = lax.axis_index("split") * block_rows + jnp.arange(block_rows, dtype=jnp.int32)
    hessian, gradient = assemble(
        softened, points[sources].astype(jnp.float32), row_seen, intersection, all_rows
    )
    hessian, gradient = in_one((hessian, gradient), "split")
    pair_cross = hessian[:, :6, 6:]
    all_poses = pose_index.shape[0]
    source_pose = pose_index[my_pairs[:, 0]]
    target_pose = pose_index[targets]
    source_part = jnp.concatenate(
        [hessian[:, :6, :6].reshape(task_count, 36), gradient[:, :6]], axis=1
    )
    target_part = jnp.concatenate(
        [hessian[:, 6:, 6:].reshape(task_count, 36), gradient[:, 6:]], axis=1
    )
    pose_slots = jnp.arange(all_poses, dtype=jnp.int32)[:, None]
    onehot_source = (pose_slots == source_pose[None, :]).astype(jnp.float32)
    onehot_target = (pose_slots == target_pose[None, :]).astype(jnp.float32)
    pose_terms = (
        jnp.dot(onehot_source, source_part, precision=highest)
        + jnp.dot(onehot_target, target_part, precision=highest)
    ) / task_count
    hessian_rows, gradient_rows = side_by_side(
        (pose_terms[:, :36], pose_terms[:, 36:]), "pair", 0, 1
    )
    return (pair_cross, hessian_rows.reshape(-1, 6, 6), gradient_rows)


def solution(mesh):
    in_specs = (
        P("pair", "split", None),
        P("pair", None, "split"),
        P("pair", None, "split"),
        P(),
        P("pair"),
        P(),
    )
    out_specs = (P("pair", None, None), P("pair", None, None), P("pair", None))
    return jax.shard_map(
        per_device, mesh=mesh, in_specs=in_specs, out_specs=out_specs, check_vma=False
    )
```

profile of v0, /device:TPU:1, one launch (start us, length us, event | category | flops | bytes accessed | tf_op | source)
XLA Modules:
  0.0 201.5 jit_solution(15148078323751725928)
XLA Ops:
  8.1 0.8 copy.64
  9.7 46.9 %all_gather.11 = bf16[64,6,128]{2,1,0:T(8,128)(2,1)S(1)} all-gather(bf16[1,6,128]{2,1,0:T(8,128)(2,1)S(1)} %pad_maximum_fusion.3), channel_id=1, replica_groups=mesh['pair'=64,'split'=8] {'pair'}, dimensions={0}, use_global_device_ids=true | all-gather | bytes 99840 | tf_op jit(solution)/shard_map/all_gather | solution.py:113
  56.6 0.9 pad_maximum_fusion.1
  57.4 24.7 %all_gather.9 = bf16[1024,259]{1,0:T(8,128)(2,1)S(1)} all-gather(bf16[128,259]{1,0:T(8,128)(2,1)S(1)} %pad_maximum_fusion.1), channel_id=1, replica_groups=mesh['pair'=64,'split'=8] {'split'}, dimensions={0}, use_global_device_ids=true | all-gather | bytes 596736 | tf_op jit(solution)/shard_map/all_gather | solution.py:12
  82.1 17.0 %all-gather.2.cloned.1.call-done = bf16[64,128,256]{2,1,0:T(8,128)(2,1)} async-done(((bf16[1,128,256]{2,1,0:T(8,128)(2,1)}), bf16[64,128,256]{2,1,0:T(8,128)(2,1)}) %all-gather.2.cloned.1.call-update) | async-done | bytes 4194320 | tf_op jit(solution)/shard_map/all_gather | solution.py:112
  99.1 37.8 %while.15 = (s32[]{:T(128)}, f32[6,4,1024]{2,1,0:T(4,128)S(1)}, f32[6,4,1024]{2,1,0:T(4,128)S(1)}, f32[6,4,6,1024]{3,2,1,0:T(8,128)}, bf16[1,1024,256]{2,1,0:T(8...) while((s32[]{:T(128)}, f32[6,4,1024]{2,1,0:T(4,128)S(1)}, ...), condition=%wide.region_3.4_spmd.clone, body=%wide.region_0.3_spmd.clone.sunk | while | flops 309847040 | bytes 7887541 | solution.py:133
  99.2 2.7 %gather_fusion = bf16[4,128,256]{2,1,0:T(8,128)(2,1)S(1)} fusion(bf16[64,128,256]{2,1,0:T(8,128)(2,1)} %get-tuple-element.215, s32[1024]{0:T(1024)S(1)} %pad_clamp_fusion.4), kind=kCustom, calls=%fused_computation.clone.1 | custom fusion | bytes 524304 | tf_op jit(solution)/shard_map/while/body/eval_jaxpr/gather | solution.py:121
  101.9 0.8 bitcast_reduce_fusion.2
  103.3 1.7 fusion.60
  105.5 2.8 %gather_fusion = bf16[4,128,256]{2,1,0:T(8,128)(2,1)S(1)} fusion(bf16[64,128,256]{2,1,0:T(8,128)(2,1)} %get-tuple-element.215, s32[1024]{0:T(1024)S(1)} %pad_clamp_fusion.4), kind=kCustom, calls=%fused_computation.clone.1 | custom fusion | bytes 524304 | tf_op jit(solution)/shard_map/while/body/eval_jaxpr/gather | solution.py:121
  108.2 0.8 bitcast_reduce_fusion.2
  109.6 1.7 fusion.60
  111.8 2.8 %gather_fusion = bf16[4,128,256]{2,1,0:T(8,128)(2,1)S(1)} fusion(bf16[64,128,256]{2,1,0:T(8,128)(2,1)} %get-tuple-element.215, s32[1024]{0:T(1024)S(1)} %pad_clamp_fusion.4), kind=kCustom, calls=%fused_computation.clone.1 | custom fusion | bytes 524304 | tf_op jit(solution)/shard_map/while/body/eval_jaxpr/gather | solution.py:121
  114.5 0.8 bitcast_reduce_fusion.2
  115.9 1.7 fusion.60
  118.1 2.8 %gather_fusion = bf16[4,128,256]{2,1,0:T(8,128)(2,1)S(1)} fusion(bf16[64,128,256]{2,1,0:T(8,128)(2,1)} %get-tuple-element.215, s32[1024]{0:T(1024)S(1)} %pad_clamp_fusion.4), kind=kCustom, calls=%fused_computation.clone.1 | custom fusion | bytes 524304 | tf_op jit(solution)/shard_map/while/body/eval_jaxpr/gather | solution.py:121
  120.8 0.8 bitcast_reduce_fusion.2
  122.2 1.7 fusion.60
  124.4 2.8 %gather_fusion = bf16[4,128,256]{2,1,0:T(8,128)(2,1)S(1)} fusion(bf16[64,128,256]{2,1,0:T(8,128)(2,1)} %get-tuple-element.215, s32[1024]{0:T(1024)S(1)} %pad_clamp_fusion.4), kind=kCustom, calls=%fused_computation.clone.1 | custom fusion | bytes 524304 | tf_op jit(solution)/shard_map/while/body/eval_jaxpr/gather | solution.py:121
  127.1 0.8 bitcast_reduce_fusion.2
  128.5 1.7 fusion.60
  130.7 2.8 %gather_fusion = bf16[4,128,256]{2,1,0:T(8,128)(2,1)S(1)} fusion(bf16[64,128,256]{2,1,0:T(8,128)(2,1)} %get-tuple-element.215, s32[1024]{0:T(1024)S(1)} %pad_clamp_fusion.4), kind=kCustom, calls=%fused_computation.clone.1 | custom fusion | bytes 524304 | tf_op jit(solution)/shard_map/while/body/eval_jaxpr/gather | solution.py:121
  133.4 0.8 bitcast_reduce_fusion.2
  134.9 1.7 fusion.60
  137.0 1.3 reshape.208
  138.4 1.0 copy.66
  139.4 9.2 %all-to-all-start = ((f32[24,8,8,128]{3,0,1,2:T(8,128)}), f32[24,8,8,128]{3,0,1,2:T(8,128)S(1)}, u32[]{:S(2)}, u32[]{:S(2)}) async-start(f32[24,8,8,128]{3,0,1,2:T(8,128)} %copy.66), calls=%async_computation | async-start | bytes 1572864 | tf_op jit(solution)/shard_map/all_to_all | solution.py:28
  148.8 12.0 %all-to-all-done = f32[24,8,8,128]{3,0,1,2:T(8,128)S(1)} async-done(((f32[24,8,8,128]{3,0,1,2:T(8,128)}), f32[24,8,8,128]{3,0,1,2:T(8,128)S(1)}, u32[]{:S(2)}, u32[]{:S(2)}) %all-to-all-start) | async-done | bytes 786464 | tf_op jit(solution)/shard_map/all_to_all | solution.py:28
  162.9 4.2 %all-to-all-start.1 = ((f32[8,1,3744]{2,1,0:T(1,128)}), f32[8,1,3744]{2,1,0:T(1,128)S(1)}, u32[]{:S(2)}, u32[]{:S(2)}) async-start(f32[8,1,3744]{2,1,0:T(1,128)} %broadcast_in_dim.20), calls=%async_computation.1 | async-start | bytes 245760 | tf_op jit(solution)/shard_map/all_to_all | solution.py:37
  168.6 3.8 %all-to-all-done.1 = f32[8,1,3744]{2,1,0:T(1,128)S(1)} async-done(((f32[8,1,3744]{2,1,0:T(1,128)}), f32[8,1,3744]{2,1,0:T(1,128)S(1)}, u32[]{:S(2)}, u32[]{:S(2)}) %all-to-all-start.1) | async-done | bytes 119840 | tf_op jit(solution)/shard_map/all_to_all | solution.py:37
  174.4 8.0 %all-to-all-start.2 = ((f32[64,1,42]{2,1,0:T(1,128)}), f32[64,1,42]{2,1,0:T(1,128)S(1)}, u32[]{:S(2)}, u32[]{:S(2)}) async-start(f32[64,1,42]{2,1,0:T(1,128)} %copy.75), calls=%async_computation.2 | async-start | bytes 65536 | tf_op jit(solution)/shard_map/all_to_all | solution.py:60
  183.2 10.1 %all-to-all-done.2 = f32[64,1,42]{2,1,0:T(1,128)S(1)} async-done(((f32[64,1,42]{2,1,0:T(1,128)}), f32[64,1,42]{2,1,0:T(1,128)S(1)}, u32[]{:S(2)}, u32[]{:S(2)}) %all-to-all-start.2) | async-done | bytes 10784 | tf_op jit(solution)/shard_map/all_to_all | solution.py:60
  (96 shorter events, 15.2 us)
Async XLA Ops:
  7.2 0.8 copy-start
  7.2 92.0 %all-gather.2.cloned.1.call-start = ((), (), s32[]{:S(2)}) async-start(), calls=%async_computation.3 | async-start | bytes 4259840 | tf_op jit(solution)/shard_map/all_gather | solution.py:112
  138.3 10.3 %copy-start.2 = (bf16[1,3,128]{2,1,0:T(4,128)(2,1)S(1)}, bf16[1,3,128]{2,1,0:T(4,128)(2,1)}, u32[]{:S(2)}) copy-start(bf16[1,3,128]{2,1,0:T(4,128)(2,1)} %param.9) | copy-start | bytes 2308
  138.4 10.4 %copy-start.3 = (s32[24]{0:T(128)S(1)}, s32[24]{0:T(128)}, u32[]{:S(2)}) copy-start(s32[24]{0:T(128)} %param.12) | copy-start | bytes 292
  139.4 21.4 %all-to-all-start = ((f32[24,8,8,128]{3,0,1,2:T(8,128)}), f32[24,8,8,128]{3,0,1,2:T(8,128)S(1)}, u32[]{:S(2)}, u32[]{:S(2)}) async-start(f32[24,8,8,128]{3,0,1,2:T(8,128)} %copy.66), calls=%async_computation | async-start | bytes 1572864 | tf_op jit(solution)/shard_map/all_to_all | solution.py:28
  148.7 18.5 %copy-start.1 = (s32[64]{0:T(128)S(1)}, s32[64]{0:T(128)}, u32[]{:S(2)}) copy-start(s32[64]{0:T(128)} %param.13) | copy-start | bytes 772
  162.9 9.4 %all-to-all-start.1 = ((f32[8,1,3744]{2,1,0:T(1,128)}), f32[8,1,3744]{2,1,0:T(1,128)S(1)}, u32[]{:S(2)}, u32[]{:S(2)}) async-start(f32[8,1,3744]{2,1,0:T(1,128)} %broadcast_in_dim.20), calls=%async_computation.1 | async-start | bytes 245760 | tf_op jit(solution)/shard_map/all_to_all | solution.py:37
  174.4 18.9 %all-to-all-start.2 = ((f32[64,1,42]{2,1,0:T(1,128)}), f32[64,1,42]{2,1,0:T(1,128)S(1)}, u32[]{:S(2)}, u32[]{:S(2)}) async-start(f32[64,1,42]{2,1,0:T(1,128)} %copy.75), calls=%async_computation.2 | async-start | bytes 65536 | tf_op jit(solution)/shard_map/all_to_all | solution.py:60
Sparse Core Ops, SparseCore 0:
  11.1 88.0 all-gather.1
where the time goes:
time: 202 us
  blocking collectives  71.6 us (35%)
  waiting for transfers between devices  43.6 us (22%)
  local copies, waits for them, and re-layouts  29.3 us (15%)
  starting transfers between devices  21.5 us (11%)
  matrix products  16.4 us (8%)
  between operations  14.4 us (7%)
  other arithmetic  4.44 us (2%)
    all_gather x1, blocking collectives, per_device(): lax.all_gather(geometry, 'pair', axis=0, tiled=True)  46.9 us
    all_gather x1, blocking collectives, rows_first(): out, at, gathered = (lax.all_gather(both, axis, axis=0, tiled=True), 0, [])  24.7 us
    all_gather x1, waiting for transfers between devices, per_device(): lax.all_gather(descriptors, 'pair', axis=0, tiled=True)  17 us
    gather x6, local copies, waits for them, and re-layouts, attend(): key_rows = target_desc[tile_ids]  16.5 us
    all_to_all x1, waiting for transfers between devices, sent_together(): lax.all_to_all(both, axis, split_axis=split_dim, concat_axis=concat_dim,...  12 us
    dot_general x6, matrix products, attend(): jnp.einsum('gij,gdj->gdi', exponent, tile_geometry, precision=highest)  10.2 us
    all_to_all x1, waiting for transfers between devices, sent_and_summed(): lax.all_to_all(pieces, axis, split_axis=0, concat_axis=0, tiled=True)  10.1 us
    all_to_all x1, starting transfers between devices, sent_together(): lax.all_to_all(both, axis, split_axis=split_dim, concat_axis=concat_dim,...  9.23 us
  transfers between devices with their start and end apart: 4, of which 4 were waited for; matrix products, arithmetic and copies ran while one was open for 2% of the time, Pallas kernels for 0%

commit v1 on v0

--- a/solution.py
+++ b/solution.py
@@ -4,6 +4,18 @@
 from jax.sharding import PartitionSpec as P
 
 task_group = 4
+
+
+def collect(array, axis, dim):
+    ways, here, step = (lax.axis_size(axis), lax.axis_index(axis), array.shape[dim])
+    line, have = (array, 1)
+    while have < ways:
+        line = jnp.concatenate(
+            [line, lax.ppermute(line, axis, [(d, (d - have) % ways) for d in range(ways)])],
+            axis=dim,
+        )
+        have = 2 * have
+    return jnp.roll(line, here * step, axis=dim)
 
 
 def rows_first(arrays, axis, dims):
@@ -110,7 +122,7 @@
     source_desc, source_points = rows_first((descriptors, points), "split", (1, 2))
     target_desc, target_geometry = (
         lax.all_gather(descriptors, "pair", axis=0, tiled=True),
-        lax.all_gather(geometry, "pair", axis=0, tiled=True),
+        collect(geometry, "pair", 0),
     )
     score_scale = feature_width ** (-0.5)
     group_count = task_count // task_group

time: 202 us -> 203 us (level)
  blocking collectives: 71.6 us -> 14.5 us
  starting transfers between devices: 21.5 us -> 51 us
  waiting for transfers between devices: 43.6 us -> 71 us
    all_gather x1 -> x0, blocking collectives: 46.9 us -> none  [per_device(): lax.all_gather(geometry, 'pair', axis=0, tiled=True)]
    ppermute x0 -> x6, starting transfers between devices: none -> 30.3 us  [collect(): lax.ppermute(line, axis, [(d, (d - have) % ways) for d in range(ways)])]
    ppermute x0 -> x6, waiting for transfers between devices: none -> 16.3 us  [collect(): lax.ppermute(line, axis, [(d, (d - have) % ways) for d in range(ways)])]
    all_gather x1, waiting for transfers between devices: 17 us -> 28 us  [per_device(): lax.all_gather(descriptors, 'pair', axis=0, tiled=True)]
    all_gather x1, blocking collectives: 24.7 us -> 14.5 us  [rows_first(): out, at, gathered = (lax.all_gather(both, axis, axis=0, tiled=True), 0, [])]
  transfers between devices with their start and end apart: 4 -> 10, of which waited for: 4 -> 9; matrix products, arithmetic and copies ran while one was open for 2% -> 2% of each run, Pallas kernels for 0% -> 0%
where the time goes in v1:
time: 203 us; the launch traced here: 202 us
  waiting for transfers between devices  71 us (35%)
  starting transfers between devices  51 us (25%)
  local copies, waits for them, and re-layouts  29.5 us (15%)
  matrix products  16.5 us (8%)
  blocking collectives  14.5 us (7%)
  between operations  14.5 us (7%)
  other arithmetic  4.48 us (2%)
    ppermute x6, starting transfers between devices, collect(): lax.ppermute(line, axis, [(d, (d - have) % ways) for d in range(ways)])  30.3 us
    all_gather x1, waiting for transfers between devices, per_device(): lax.all_gather(descriptors, 'pair', axis=0, tiled=True)  28 us
    gather x6, local copies, waits for them, and re-layouts, attend(): key_rows = target_desc[tile_ids]  16.5 us
    ppermute x6, waiting for transfers between devices, collect(): lax.ppermute(line, axis, [(d, (d - have) % ways) for d in range(ways)])  16.3 us
    all_gather x1, blocking collectives, rows_first(): out, at, gathered = (lax.all_gather(both, axis, axis=0, tiled=True), 0, [])  14.5 us
    all_to_all x1, waiting for transfers between devices, sent_together(): lax.all_to_all(both, axis, split_axis=split_dim, concat_axis=concat_dim,...  12 us
    dot_general x6, matrix products, attend(): jnp.einsum('gij,gdj->gdi', exponent, tile_geometry, precision=highest)  10.3 us
    all_to_all x1, waiting for transfers between devices, sent_and_summed(): lax.all_to_all(pieces, axis, split_axis=0, concat_axis=0, tiled=True)  10.2 us
  transfers between devices with their start and end apart: 10, of which 9 were waited for; matrix products, arithmetic and copies ran while one was open for 2% of the time, Pallas kernels for 0%

profile of v1, /device:TPU:1, one launch (start us, length us, event | category | flops | bytes accessed | tf_op | source)
XLA Modules:
  0.0 201.7 jit_solution(2899176254808171923)
XLA Ops:
  8.6 14.4 %collective-permute-start = (bf16[1,6,128]{2,1,0:T(8,128)(2,1)S(1)}, bf16[1,6,128]{2,1,0:T(8,128)(2,1)S(1)}, u32[]{:S(2)}, u32[]{:S(2)}) collective-permute-start(bf16[1,6,128]{2,1,0:T(8,128)(2,1)S(1)} %get-tuple-element.144), channel_id=1, source_target_pairs={{0,504},{8,0},{16,8},{24,16},{32,24},{40,32},{48,40},{56,48},{64,5... | collective-permute-start | bytes 4616 | tf_op jit(solution)/shard_map/ppermute | solution.py:14
  24.7 14.5 %all_gather.6 = bf16[1024,259]{1,0:T(8,128)(2,1)S(1)} all-gather(bf16[128,259]{1,0:T(8,128)(2,1)S(1)} %pad_maximum_fusion.1), channel_id=1, replica_groups=mesh['pair'=64,'split'=8] {'split'}, dimensions={0}, use_global_device_ids=true | all-gather | bytes 596736 | tf_op jit(solution)/shard_map/all_gather | solution.py:24
  39.3 3.8 %collective-permute-start.1 = (bf16[2,6,128]{2,1,0:T(8,128)(2,1)S(1)}, bf16[2,6,128]{2,1,0:T(8,128)(2,1)S(1)}, u32[]{:S(2)}, u32[]{:S(2)}) collective-permute-start(bf16[2,6,128]{2,1,0:T(8,128)(2,1)S(1)} %pad_maximum_fusion.5), channel_id=1, source_target_pairs={{0,496},{8,504},{16,0},{24,8},{32,16},{40,24},{48,32},{56,40},{64,... | collective-permute-start | bytes 9224 | tf_op jit(solution)/shard_map/ppermute | solution.py:14
  43.1 1.5 collective-permute-done.1
  44.6 4.8 %collective-permute-start.2 = (bf16[4,6,128]{2,1,0:T(8,128)(2,1)S(1)}, bf16[4,6,128]{2,1,0:T(8,128)(2,1)S(1)}, u32[]{:S(2)}, u32[]{:S(2)}) collective-permute-start(bf16[4,6,128]{2,1,0:T(8,128)(2,1)S(1)} %pad_maximum_fusion.4), channel_id=1, source_target_pairs={{0,480},{8,488},{16,496},{24,504},{32,0},{40,8},{48,16},{56,24},{6... | collective-permute-start | bytes 18440 | tf_op jit(solution)/shard_map/ppermute | solution.py:14
  49.4 3.5 %collective-permute-done.2 = bf16[4,6,128]{2,1,0:T(8,128)(2,1)S(1)} collective-permute-done((bf16[4,6,128]{2,1,0:T(8,128)(2,1)S(1)}, bf16[4,6,128]{2,1,0:T(8,128)(2,1)S(1)}, u32[]{:S(2)}, u32[]{:S(2)}) %collective-permute-start.2) | collective-permute-done | bytes 6176 | tf_op jit(solution)/shard_map/ppermute | solution.py:14
  52.9 2.1 %collective-permute-start.3 = (bf16[8,6,128]{2,1,0:T(8,128)(2,1)S(1)}, bf16[8,6,128]{2,1,0:T(8,128)(2,1)S(1)}, u32[]{:S(2)}, u32[]{:S(2)}) collective-permute-start(bf16[8,6,128]{2,1,0:T(8,128)(2,1)S(1)} %pad_maximum_fusion.2), channel_id=1, source_target_pairs={{0,448},{8,456},{16,464},{24,472},{32,480},{40,488},{48,496},{56,5... | collective-permute-start | bytes 36872 | tf_op jit(solution)/shard_map/ppermute | solution.py:14
  55.1 2.3 %collective-permute-done.3 = bf16[8,6,128]{2,1,0:T(8,128)(2,1)S(1)} collective-permute-done((bf16[8,6,128]{2,1,0:T(8,128)(2,1)S(1)}, bf16[8,6,128]{2,1,0:T(8,128)(2,1)S(1)}, u32[]{:S(2)}, u32[]{:S(2)}) %collective-permute-start.3) | collective-permute-done | bytes 12320 | tf_op jit(solution)/shard_map/ppermute | solution.py:14
  57.4 2.6 %collective-permute-start.4 = (bf16[16,6,128]{2,1,0:T(8,128)(2,1)S(1)}, bf16[16,6,128]{2,1,0:T(8,128)(2,1)S(1)}, u32[]{:S(2)}, u32[]{:S(2)}) collective-permute-start(bf16[16,6,128]{2,1,0:T(8,128)(2,1)S(1)} %get-tuple-element.126), channel_id=1, source_target_pairs={{0,384},{8,392},{16,400},{24,408},{32,416},{40,424},{48,432},{56,4... | collective-permute-start | bytes 73736 | tf_op jit(solution)/shard_map/ppermute | solution.py:14
  60.1 2.9 %collective-permute-done.4 = bf16[16,6,128]{2,1,0:T(8,128)(2,1)S(1)} collective-permute-done((bf16[16,6,128]{2,1,0:T(8,128)(2,1)S(1)}, bf16[16,6,128]{2,1,0:T(8,128)(2,1)S(1)}, u32[]{:S(2)}, u32[]{:S(2)}) %collective-permute-start.4) | collective-permute-done | bytes 24608 | tf_op jit(solution)/shard_map/ppermute | solution.py:14
  63.0 2.7 %collective-permute-start.5 = (bf16[32,6,128]{2,1,0:T(8,128)(2,1)S(1)}, bf16[32,6,128]{2,1,0:T(8,128)(2,1)S(1)}, u32[]{:S(2)}, u32[]{:S(2)}) collective-permute-start(bf16[32,6,128]{2,1,0:T(8,128)(2,1)S(1)} %get-tuple-element.122), channel_id=1, source_target_pairs={{0,256},{8,264},{16,272},{24,280},{32,288},{40,296},{48,304},{56,3... | collective-permute-start | bytes 147464 | tf_op jit(solution)/shard_map/ppermute | solution.py:14
  65.9 6.1 %collective-permute-done.5 = bf16[32,6,128]{2,1,0:T(8,128)(2,1)S(1)} collective-permute-done((bf16[32,6,128]{2,1,0:T(8,128)(2,1)S(1)}, bf16[32,6,128]{2,1,0:T(8,128)(2,1)S(1)}, u32[]{:S(2)}, u32[]{:S(2)}) %collective-permute-start.5) | collective-permute-done | bytes 49184 | tf_op jit(solution)/shard_map/ppermute | solution.py:14
  72.1 28.0 %all-gather.2.cloned.1.call-done = bf16[64,128,256]{2,1,0:T(8,128)(2,1)} async-done(((bf16[1,128,256]{2,1,0:T(8,128)(2,1)}), bf16[64,128,256]{2,1,0:T(8,128)(2,1)}) %all-gather.2.cloned.1.call-update) | async-done | bytes 4194320 | tf_op jit(solution)/shard_map/all_gather | solution.py:124
  100.1 37.9 %while.15 = (s32[]{:T(128)}, f32[6,4,1024]{2,1,0:T(4,128)S(1)}, f32[6,4,1024]{2,1,0:T(4,128)S(1)}, f32[6,4,6,1024]{3,2,1,0:T(8,128)}, bf16[1,1024,256]{2,1,0:T(8...) while((s32[]{:T(128)}, f32[6,4,1024]{2,1,0:T(4,128)S(1)}, ...), condition=%wide.region_3.4_spmd.clone, body=%wide.region_0.3_spmd.clone.sunk | while | flops 309847040 | bytes 7887541 | solution.py:145
  100.1 2.7 %gather_fusion = bf16[4,128,256]{2,1,0:T(8,128)(2,1)S(1)} fusion(bf16[64,128,256]{2,1,0:T(8,128)(2,1)} %get-tuple-element.233, s32[1024]{0:T(1024)S(1)} %pad_clamp_fusion.4), kind=kCustom, calls=%fused_computation.clone.1 | custom fusion | bytes 524304 | tf_op jit(solution)/shard_map/while/body/eval_jaxpr/gather | solution.py:133
  104.3 1.7 fusion.59
  106.4 2.8 %gather_fusion = bf16[4,128,256]{2,1,0:T(8,128)(2,1)S(1)} fusion(bf16[64,128,256]{2,1,0:T(8,128)(2,1)} %get-tuple-element.233, s32[1024]{0:T(1024)S(1)} %pad_clamp_fusion.4), kind=kCustom, calls=%fused_computation.clone.1 | custom fusion | bytes 524304 | tf_op jit(solution)/shard_map/while/body/eval_jaxpr/gather | solution.py:133
  110.6 1.7 fusion.59
  112.8 2.8 %gather_fusion = bf16[4,128,256]{2,1,0:T(8,128)(2,1)S(1)} fusion(bf16[64,128,256]{2,1,0:T(8,128)(2,1)} %get-tuple-element.233, s32[1024]{0:T(1024)S(1)} %pad_clamp_fusion.4), kind=kCustom, calls=%fused_computation.clone.1 | custom fusion | bytes 524304 | tf_op jit(solution)/shard_map/while/body/eval_jaxpr/gather | solution.py:133
  116.9 1.7 fusion.59
  119.1 2.8 %gather_fusion = bf16[4,128,256]{2,1,0:T(8,128)(2,1)S(1)} fusion(bf16[64,128,256]{2,1,0:T(8,128)(2,1)} %get-tuple-element.233, s32[1024]{0:T(1024)S(1)} %pad_clamp_fusion.4), kind=kCustom, calls=%fused_computation.clone.1 | custom fusion | bytes 524304 | tf_op jit(solution)/shard_map/while/body/eval_jaxpr/gather | solution.py:133
  123.2 1.7 fusion.59
  125.4 2.8 %gather_fusion = bf16[4,128,256]{2,1,0:T(8,128)(2,1)S(1)} fusion(bf16[64,128,256]{2,1,0:T(8,128)(2,1)} %get-tuple-element.233, s32[1024]{0:T(1024)S(1)} %pad_clamp_fusion.4), kind=kCustom, calls=%fused_computation.clone.1 | custom fusion | bytes 524304 | tf_op jit(solution)/shard_map/while/body/eval_jaxpr/gather | solution.py:133
  129.6 1.7 fusion.59
  131.7 2.8 %gather_fusion = bf16[4,128,256]{2,1,0:T(8,128)(2,1)S(1)} fusion(bf16[64,128,256]{2,1,0:T(8,128)(2,1)} %get-tuple-element.233, s32[1024]{0:T(1024)S(1)} %pad_clamp_fusion.4), kind=kCustom, calls=%fused_computation.clone.1 | custom fusion | bytes 524304 | tf_op jit(solution)/shard_map/while/body/eval_jaxpr/gather | solution.py:133
  135.9 1.7 fusion.59
  140.5 8.9 %all-to-all-start = ((f32[24,8,8,128]{3,0,1,2:T(8,128)}), f32[24,8,8,128]{3,0,1,2:T(8,128)S(1)}, u32[]{:S(2)}, u32[]{:S(2)}) async-start(f32[24,8,8,128]{3,0,1,2:T(8,128)} %copy.66), calls=%async_computation | async-start | bytes 1572864 | tf_op jit(solution)/shard_map/all_to_all | solution.py:40
  149.5 12.0 %all-to-all-done = f32[24,8,8,128]{3,0,1,2:T(8,128)S(1)} async-done(((f32[24,8,8,128]{3,0,1,2:T(8,128)}), f32[24,8,8,128]{3,0,1,2:T(8,128)S(1)}, u32[]{:S(2)}, u32[]{:S(2)}) %all-to-all-start) | async-done | bytes 786464 | tf_op jit(solution)/shard_map/all_to_all | solution.py:40
  163.6 4.2 %all-to-all-start.1 = ((f32[8,1,3744]{2,1,0:T(1,128)}), f32[8,1,3744]{2,1,0:T(1,128)S(1)}, u32[]{:S(2)}, u32[]{:S(2)}) async-start(f32[8,1,3744]{2,1,0:T(1,128)} %broadcast_in_dim.20), calls=%async_computation.1 | async-start | bytes 245760 | tf_op jit(solution)/shard_map/all_to_all | solution.py:49
  169.3 3.8 %all-to-all-done.1 = f32[8,1,3744]{2,1,0:T(1,128)S(1)} async-done(((f32[8,1,3744]{2,1,0:T(1,128)}), f32[8,1,3744]{2,1,0:T(1,128)S(1)}, u32[]{:S(2)}, u32[]{:S(2)}) %all-to-all-start.1) | async-done | bytes 119840 | tf_op jit(solution)/shard_map/all_to_all | solution.py:49
  175.1 7.5 %all-to-all-start.2 = ((f32[64,1,42]{2,1,0:T(1,128)}), f32[64,1,42]{2,1,0:T(1,128)S(1)}, u32[]{:S(2)}, u32[]{:S(2)}) async-start(f32[64,1,42]{2,1,0:T(1,128)} %copy.75), calls=%async_computation.2 | async-start | bytes 65536 | tf_op jit(solution)/shard_map/all_to_all | solution.py:72
  183.4 10.2 %all-to-all-done.2 = f32[64,1,42]{2,1,0:T(1,128)S(1)} async-done(((f32[64,1,42]{2,1,0:T(1,128)}), f32[64,1,42]{2,1,0:T(1,128)S(1)}, u32[]{:S(2)}, u32[]{:S(2)}) %all-to-all-start.2) | async-done | bytes 10784 | tf_op jit(solution)/shard_map/all_to_all | solution.py:72
  (126 shorter events, 24.4 us)
Async XLA Ops:
  7.2 52.8 %copy-start = (s32[1536,2]{0,1:T(2,128)S(1)}, s32[1536,2]{0,1:T(2,128)}, u32[]{:S(2)}) copy-start(s32[1536,2]{0,1:T(2,128)} %param.11) | copy-start | bytes 36868
  7.2 32.1 %copy-start.3 = (bf16[1,3,128]{2,1,0:T(4,128)(2,1)S(1)}, bf16[1,3,128]{2,1,0:T(4,128)(2,1)}, u32[]{:S(2)}) copy-start(bf16[1,3,128]{2,1,0:T(4,128)(2,1)} %param.10) | copy-start | bytes 2308
  7.2 32.1 %copy-start.2 = (bf16[1,3,128]{2,1,0:T(4,128)(2,1)S(1)}, bf16[1,3,128]{2,1,0:T(4,128)(2,1)}, u32[]{:S(2)}) copy-start(bf16[1,3,128]{2,1,0:T(4,128)(2,1)} %param.9) | copy-start | bytes 2308
  7.2 92.9 %all-gather.2.cloned.1.call-start = ((), (), s32[]{:S(2)}) async-start(), calls=%async_computation.3 | async-start | bytes 4259840 | tf_op jit(solution)/shard_map/all_gather | solution.py:124
  8.6 30.6 %collective-permute-start = (bf16[1,6,128]{2,1,0:T(8,128)(2,1)S(1)}, bf16[1,6,128]{2,1,0:T(8,128)(2,1)S(1)}, u32[]{:S(2)}, u32[]{:S(2)}) collective-permute-start(bf16[1,6,128]{2,1,0:T(8,128)(2,1)S(1)} %get-tuple-element.144), channel_id=1, source_target_pairs={{0,504},{8,0},{16,8},{24,16},{32,24},{40,32},{48,40},{56,48},{64,5... | collective-permute-start | bytes 4616 | tf_op jit(solution)/shard_map/ppermute | solution.py:14
  39.3 5.3 %collective-permute-start.1 = (bf16[2,6,128]{2,1,0:T(8,128)(2,1)S(1)}, bf16[2,6,128]{2,1,0:T(8,128)(2,1)S(1)}, u32[]{:S(2)}, u32[]{:S(2)}) collective-permute-start(bf16[2,6,128]{2,1,0:T(8,128)(2,1)S(1)} %pad_maximum_fusion.5), channel_id=1, source_target_pairs={{0,496},{8,504},{16,0},{24,8},{32,16},{40,24},{48,32},{56,40},{64,... | collective-permute-start | bytes 9224 | tf_op jit(solution)/shard_map/ppermute | solution.py:14
  44.6 8.3 %collective-permute-start.2 = (bf16[4,6,128]{2,1,0:T(8,128)(2,1)S(1)}, bf16[4,6,128]{2,1,0:T(8,128)(2,1)S(1)}, u32[]{:S(2)}, u32[]{:S(2)}) collective-permute-start(bf16[4,6,128]{2,1,0:T(8,128)(2,1)S(1)} %pad_maximum_fusion.4), channel_id=1, source_target_pairs={{0,480},{8,488},{16,496},{24,504},{32,0},{40,8},{48,16},{56,24},{6... | collective-permute-start | bytes 18440 | tf_op jit(solution)/shard_map/ppermute | solution.py:14
  52.9 4.5 %collective-permute-start.3 = (bf16[8,6,128]{2,1,0:T(8,128)(2,1)S(1)}, bf16[8,6,128]{2,1,0:T(8,128)(2,1)S(1)}, u32[]{:S(2)}, u32[]{:S(2)}) collective-permute-start(bf16[8,6,128]{2,1,0:T(8,128)(2,1)S(1)} %pad_maximum_fusion.2), channel_id=1, source_target_pairs={{0,448},{8,456},{16,464},{24,472},{32,480},{40,488},{48,496},{56,5... | collective-permute-start | bytes 36872 | tf_op jit(solution)/shard_map/ppermute | solution.py:14
  57.4 5.6 %collective-permute-start.4 = (bf16[16,6,128]{2,1,0:T(8,128)(2,1)S(1)}, bf16[16,6,128]{2,1,0:T(8,128)(2,1)S(1)}, u32[]{:S(2)}, u32[]{:S(2)}) collective-permute-start(bf16[16,6,128]{2,1,0:T(8,128)(2,1)S(1)} %get-tuple-element.126), channel_id=1, source_target_pairs={{0,384},{8,392},{16,400},{24,408},{32,416},{40,424},{48,432},{56,4... | collective-permute-start | bytes 73736 | tf_op jit(solution)/shard_map/ppermute | solution.py:14
  63.0 8.9 %collective-permute-start.5 = (bf16[32,6,128]{2,1,0:T(8,128)(2,1)S(1)}, bf16[32,6,128]{2,1,0:T(8,128)(2,1)S(1)}, u32[]{:S(2)}, u32[]{:S(2)}) collective-permute-start(bf16[32,6,128]{2,1,0:T(8,128)(2,1)S(1)} %get-tuple-element.122), channel_id=1, source_target_pairs={{0,256},{8,264},{16,272},{24,280},{32,288},{40,296},{48,304},{56,3... | collective-permute-start | bytes 147464 | tf_op jit(solution)/shard_map/ppermute | solution.py:14
  139.4 10.0 %copy-start.4 = (s32[24]{0:T(128)S(1)}, s32[24]{0:T(128)}, u32[]{:S(2)}) copy-start(s32[24]{0:T(128)} %param.12) | copy-start | bytes 292
  140.5 21.1 %all-to-all-start = ((f32[24,8,8,128]{3,0,1,2:T(8,128)}), f32[24,8,8,128]{3,0,1,2:T(8,128)S(1)}, u32[]{:S(2)}, u32[]{:S(2)}) async-start(f32[24,8,8,128]{3,0,1,2:T(8,128)} %copy.66), calls=%async_computation | async-start | bytes 1572864 | tf_op jit(solution)/shard_map/all_to_all | solution.py:40
  149.4 18.5 %copy-start.1 = (s32[64]{0:T(128)S(1)}, s32[64]{0:T(128)}, u32[]{:S(2)}) copy-start(s32[64]{0:T(128)} %param.13) | copy-start | bytes 772
  163.6 9.4 %all-to-all-start.1 = ((f32[8,1,3744]{2,1,0:T(1,128)}), f32[8,1,3744]{2,1,0:T(1,128)S(1)}, u32[]{:S(2)}, u32[]{:S(2)}) async-start(f32[8,1,3744]{2,1,0:T(1,128)} %broadcast_in_dim.20), calls=%async_computation.1 | async-start | bytes 245760 | tf_op jit(solution)/shard_map/all_to_all | solution.py:49
  175.1 18.4 %all-to-all-start.2 = ((f32[64,1,42]{2,1,0:T(1,128)}), f32[64,1,42]{2,1,0:T(1,128)S(1)}, u32[]{:S(2)}, u32[]{:S(2)}) async-start(f32[64,1,42]{2,1,0:T(1,128)} %copy.75), calls=%async_computation.2 | async-start | bytes 65536 | tf_op jit(solution)/shard_map/all_to_all | solution.py:72
Sparse Core Ops, SparseCore 0:
  11.1 88.9 all-gather.1
